TPU v7x, 32 devices: a whole 2x2x4 slice. The times are simulated.
32 devices in a mesh: docs: 8 (over z, x), topics: 4 (over y, core).
Axes of the slice: x: 2, y: 2, z: 4, core: 2. Of those that a mesh axis runs over, the one named last changes fastest.
Arguments:
- log_beta: bfloat16 [262144, 2048], P('docs', 'topics'), may hold values from -250 to -4
- gamma_init: float32 [128, 2048], P('docs', 'topics'), may hold values from 0.05 to 5
- topic_prior: float32 [2048], P('topics'), may hold values from 0.02 to 0.5
- word_block: int32 [128, 256, 1], P('docs'), may hold values from 0 to 7; in each aligned block of 4096 rows (0 to 4095, 4096 to 8191, ..., all dimensions but the last counted through in order) at most 1024 rows name the same one
- word_row: int32 [128, 256], P('docs'), may hold values from 0 to 32767
- counts: int32 [128, 256], P('docs'), may hold values from 0 to 2
Outputs:
- doc_gamma: float32 [128, 2048], P('docs', 'topics')
- sstats: float32 [262144, 2048], P('docs', 'topics')
Inputs may be any that keep to these rules, and one draw needn't show every extreme that they name: `word_block`: among the token slots of one device's 16 documents, at most 1024 name the same vocabulary block, and some block is named by exactly 1024 of them on some device. `counts`: A count of 0 marks an empty slot.
All inputs are finite; a program needn't handle non-finite values.
Results may differ from a plain program's by a relative error of at most 0.0003.
Values may be sent and summed in bfloat16 or wider, within the bound.
A program may use at most 192 MiB of HBM per device.

v0:
```python
import functools

import jax
import jax.numpy as jnp
from jax import lax
from jax.experimental import pallas as pl
from jax.experimental.pallas import tpu as pltpu
from jax.sharding import PartitionSpec as P

ITERS = 3
MESH = pl.DeviceIdType.MESH
LANES = 256
DEEP = 2048
PIECE = 128
SUB = 256
STEP = 16
HALVES = 2
GATHER_LIMIT = 16 * 1024 * 1024
SWEEP_LIMIT = 12 * 1024 * 1024
STATS_LIMIT = 16 * 1024 * 1024


def share_kernel(owners, vocab, packed_ref, key_ref, seen, send, recv):
    me, part = lax.axis_index("docs"), lax.axis_index("topics")
    doc_rows = packed_ref.shape[0]
    all_docs = owners * doc_rows

    def owner(i):
        return lax.rem(me + i, owners)

    barrier = pltpu.get_barrier_semaphore()
    for i in range(1, owners):
        pl.semaphore_signal(barrier, inc=1, device_id=(owner(i), part), device_id_type=MESH)
    pl.semaphore_wait(barrier, owners - 1)

    def copy(i):
        return pltpu.make_async_remote_copy(
            src_ref=packed_ref, dst_ref=seen.at[me], send_sem=send.at[i], recv_sem=recv.at[i],
            device_id=(owner(i), part), device_id_type=MESH,
        )

    for i in range(1, owners):
        copy(i).start()
    seen[me] = packed_ref[...]
    for i in range(1, owners):
        copy(i).wait()
    holder = lax.broadcasted_iota(jnp.int32, packed_ref.shape, 0)
    for o in range(owners):
        token = seen[o]
        count, word = token & 3, token >> 2
        row = word - me * vocab
        ours = (count > 0) & (row >= 0) & (row < vocab)
        key = (row * all_docs + (holder + o * doc_rows)) * 4 + count
        key_ref[o * doc_rows:(o + 1) * doc_rows, :] = jnp.where(ours, key, vocab * all_docs * 4)


def share_tokens(packed, vocab):
    owners, (doc_rows, length) = lax.axis_size("docs"), packed.shape
    vmem = pl.BlockSpec(memory_space=pltpu.VMEM)
    return pl.pallas_call(
        functools.partial(share_kernel, owners, vocab),
        out_shape=jax.ShapeDtypeStruct((owners * doc_rows, length), jnp.int32),
        in_specs=[vmem],
        out_specs=vmem,
        scratch_shapes=[
            pltpu.VMEM((owners, doc_rows, length), jnp.int32),
            pltpu.SemaphoreType.DMA((owners,)),
            pltpu.SemaphoreType.DMA((owners,)),
        ],
        compiler_params=pltpu.CompilerParams(collective_id=1, has_side_effects=True),
    )(packed)


def make_windows(row_ref, table):
    lines = row_ref.shape[0] - 8
    here, after = row_ref[:lines, :], row_ref[1:lines + 1, :]
    lane = lax.broadcasted_iota(jnp.int32, here.shape, 1)
    table[:lines, :] = here
    for k in range(1, PIECE // STEP):
        back = PIECE - k * STEP
        table[k * lines:(k + 1) * lines, :] = jnp.where(
            lane < back, pltpu.roll(here, back, 1), pltpu.roll(after, back, 1)
        )


def window_rows(table, start):
    lines = table.shape[0] * STEP // PIECE
    place = lax.rem(start, PIECE) // STEP * lines + start // PIECE
    return table[pl.ds(place, 1), :]


def gather_kernel(bound_ref, row_ref, beta_ref, out_ref, table, held, sems):
    depth, height, cols = held.shape
    steps = beta_ref.shape[0] // height
    parts = height // SUB

    def copy(s):
        slot = lax.rem(s, depth)
        rows = pl.ds(pl.multiple_of(s * height, height), height)
        return pltpu.make_async_copy(beta_ref.at[rows], held.at[slot], sems.at[slot])

    for s in range(depth):
        copy(s).start()
    make_windows(row_ref, table)
    out_ref[...] = jnp.zeros_like(out_ref)
    lane_row = lax.broadcasted_iota(jnp.int32, (SUB, PIECE), 0)

    def fetch(s, part, start):
        base = (s * parts + part) * SUB
        hit = jnp.where(lane_row == window_rows(table, start) - base, 1.0, 0.0).astype(jnp.bfloat16)
        rows = tn(hit, held[lax.rem(s, depth), part * SUB:(part + 1) * SUB, :])
        place = pl.ds(pl.multiple_of(start, STEP), PIECE)
        out_ref[place, :] = (out_ref[place, :].astype(jnp.float32) + rows).astype(out_ref.dtype)

    def step(s, carry):
        copy(s).wait()
        firsts = []
        for part in range(parts):
            firsts.append(bound_ref[s * parts + part] // STEP * STEP)
            fetch(s, part, firsts[-1])
        for part in range(parts):
            end = bound_ref[s * parts + part + 1]

            def more(i, carry, part=part):
                fetch(s, part, firsts[part] + i * PIECE)
                return carry

            lax.fori_loop(1, (end - firsts[part] + PIECE - 1) // PIECE, more, 0)

        @pl.when(s + depth < steps)
        def _():
            copy(s + depth).start()

        return carry

    lax.fori_loop(0, steps, step, 0)


def gather_rows(log_beta, rows, bounds):
    (total, cols), slots = log_beta.shape, (rows.shape[0] - 8) * PIECE
    height = 1024
    depth = min(8, total // height)
    return pl.pallas_call(
        gather_kernel,
        out_shape=jax.ShapeDtypeStruct((slots + PIECE, cols), log_beta.dtype),
        in_specs=[
            pl.BlockSpec(memory_space=pltpu.SMEM),
            pl.BlockSpec(memory_space=pltpu.VMEM),
            pl.BlockSpec(memory_space=pl.ANY),
        ],
        out_specs=pl.BlockSpec(memory_space=pltpu.VMEM),
        scratch_shapes=[
            pltpu.VMEM((slots // STEP, PIECE), jnp.int32),
            pltpu.VMEM((depth, height, cols), log_beta.dtype),
            pltpu.SemaphoreType.DMA((depth,)),
        ],
        compiler_params=pltpu.CompilerParams(vmem_limit_bytes=GATHER_LIMIT),
    )(bounds, rows, log_beta)


def nt(a, b):
    return lax.dot_general(a, b, (((1,), (1,)), ((), ())), preferred_element_type=jnp.float32)


def tn(a, b):
    return lax.dot_general(a, b, (((0,), (0,)), ((), ())), preferred_element_type=jnp.float32)


def nn(a, b):
    return jnp.dot(a, b, preferred_element_type=jnp.float32)


def split(x):
    high = x.astype(jnp.bfloat16)
    return high, (x - high.astype(jnp.float32)).astype(jnp.bfloat16)


def digamma(x):
    top, bottom = jnp.ones_like(x), x
    for i in range(1, 8):
        top = top * (x + i) + bottom
        bottom = bottom * (x + i)
    y = x + 8.0
    inv = 1.0 / y
    sq = inv * inv
    series = sq * (1.0 / 12 - sq * (1.0 / 120 - sq * (1.0 / 252)))
    return jnp.log(y) - 0.5 * inv - series - top / bottom


def sweep_kernel(
    owners, parts, found_ref, doc_ref, count_ref, gamma_ref, prior_ref,
    gamma_out, high, low,
    weights, theta_two, placed, sums, theta_all, theta_mine, sums_in, tops, norms, scale,
    theta_send, theta_recv, sums_send, sums_recv, top_send, top_recv, norm_send, norm_recv,
):
    me, part = lax.axis_index("docs"), lax.axis_index("topics")
    lines = doc_ref.shape[0]
    tokens, cols = lines * LANES, high.shape[1]
    doc_rows = gamma_ref.shape[0]
    docs = owners * doc_rows
    half = cols // HALVES
    block = DEEP // LANES
    blocks = tokens // DEEP
    others = sorted(range(1, owners), key=lambda i: abs(2 * i - owners))

    def owner(i):
        return lax.rem(me + i, owners)

    def fellow(i):
        return lax.rem(part + i, parts)

    barrier = pltpu.get_barrier_semaphore()
    for i in others:
        pl.semaphore_signal(barrier, inc=1, device_id=(owner(i), part), device_id_type=MESH)
    for i in range(1, parts):
        pl.semaphore_signal(barrier, inc=1, device_id=(me, fellow(i)), device_id_type=MESH)

    mine = pl.ds(pl.multiple_of(me * doc_rows, doc_rows), doc_rows)

    def side(h):
        return slice(h * half, (h + 1) * half)

    def theta_copy(h, i):
        return pltpu.make_async_remote_copy(
            src_ref=theta_mine.at[h], dst_ref=theta_all.at[h, mine],
            send_sem=theta_send.at[h, i], recv_sem=theta_recv.at[h, i],
            device_id=(owner(i), part), device_id_type=MESH,
        )

    def sums_copy(h, i):
        theirs = pl.ds(pl.multiple_of(owner(i) * doc_rows, doc_rows), doc_rows)
        return pltpu.make_async_remote_copy(
            src_ref=sums.at[h, theirs], dst_ref=sums_in.at[h, i],
            send_sem=sums_send.at[h, i], recv_sem=sums_recv.at[h, i],
            device_id=(owner(i), part), device_id_type=MESH,
        )

    def top_copy(i):
        return pltpu.make_async_remote_copy(
            src_ref=tops.at[0], dst_ref=tops.at[i], send_sem=top_send.at[i], recv_sem=top_recv.at[i],
            device_id=(me, fellow(i)), device_id_type=MESH,
        )

    def norm_copy(i, turn, q):
        piece = pl.ds(pl.multiple_of(q * block, block), block)
        return pltpu.make_async_remote_copy(
            src_ref=norms.at[turn, 0, piece], dst_ref=norms.at[turn, i, piece],
            send_sem=norm_send.at[turn, i, q], recv_sem=norm_recv.at[turn, i, q],
            device_id=(me, fellow(i)), device_id_type=MESH,
        )

    def send_theta(h, gamma):
        theta_mine[h] = jnp.exp(digamma(gamma))
        for i in others:
            theta_copy(h, i).start()
        theta_all[h, mine, :] = theta_mine[h]

    pl.semaphore_wait(barrier, owners + parts - 2)
    for h in range(HALVES):
        send_theta(h, gamma_ref[:, side(h)])

    pick = jnp.where(lax.broadcasted_iota(jnp.int32, (16, PIECE), 1) == 0, 1.0, 0.0).astype(jnp.bfloat16)

    def make_mass(c, carry):
        rows = pl.ds(pl.multiple_of(c * LANES, LANES), LANES)
        x = found_ref[rows, :].astype(jnp.float32)
        top = jnp.max(x, axis=1, keepdims=True)
        high[rows, :], low[rows, :] = split(jnp.exp(x - top))
        wide = jnp.broadcast_to(top, (LANES, PIECE)).astype(jnp.bfloat16)
        tops[0, pl.ds(c, 1), :] = nt(pick, wide)[:1]
        return carry

    lax.fori_loop(0, lines, make_mass, 0, unroll=4)
    for i in range(1, parts):
        top_copy(i).start()

    lane_doc = lax.broadcasted_iota(jnp.int32, (docs, LANES), 0)

    def deep_rows(q):
        return pl.ds(pl.multiple_of(q * DEEP, DEEP), DEEP)

    def block_lines(q):
        return pl.ds(pl.multiple_of(q * block, block), block)

    def products(turn):
        def step(q, carry):
            both = nt(theta_two[...], high[deep_rows(q), :])
            less = nt(theta_two[:docs, :], low[deep_rows(q), :])
            total = both[:docs] + both[docs:] + less
            for j in range(block):
                line = pl.ds(q * block + j, 1)
                chosen = jnp.where(lane_doc == doc_ref[line, :], total[:, j * LANES:(j + 1) * LANES], 0.0)
                norms[turn, 0, line, :] = jnp.sum(chosen, axis=0, keepdims=True)
            for i in range(1, parts):
                norm_copy(i, turn, q).start()
            return carry

        lax.fori_loop(0, blocks, step, 0)

    def new_weights(turn, q):
        piece = block_lines(q)
        for i in range(1, parts):
            norm_copy(i, turn, q).wait()
        norm = scale[0, piece, :] * norms[turn, 0, piece, :]
        for i in range(1, parts):
            norm = norm + scale[i, piece, :] * norms[turn, i, piece, :]
        weights[piece, :] = count_ref[piece, :] * scale[0, piece, :] / norm

    def add_sums(h, q):
        both = nn(placed[q], high[deep_rows(q), side(h)])
        less = nn(placed[q, :docs], low[deep_rows(q), side(h)])
        sums[h] += both[:docs] + both[docs:] + less

    def first_sums(turn):
        def step(q, carry):
            new_weights(turn, q)
            for j in range(block):
                line = pl.ds(q * block + j, 1)
                h, l = split(jnp.where(lane_doc == doc_ref[line, :], weights[line, :], 0.0))
                placed[q, :docs, j * LANES:(j + 1) * LANES] = h
                placed[q, docs:, j * LANES:(j + 1) * LANES] = l
            add_sums(0, q)
            return carry

        lax.fori_loop(0, blocks, step, 0)

    def later_sums(h):
        def step(q, carry):
            add_sums(h, q)
            return carry

        lax.fori_loop(0, blocks, step, 0)

    def spread(c, carry):
        rows = pl.ds(pl.multiple_of(c * LANES, LANES), LANES)
        wh, wl = split(jnp.where(lane_doc == doc_ref[pl.ds(c, 1), :], weights[pl.ds(c, 1), :], 0.0))
        theta = tn(jnp.concatenate([wh, wh], axis=0), theta_two[...]) + tn(wl, theta_two[:docs, :])
        mass = high[rows, :].astype(jnp.float32) + low[rows, :].astype(jnp.float32)
        high[rows, :], low[rows, :] = split(mass * theta)
        return carry

    for sweep in range(ITERS + 1):
        turn = sweep % 2
        for h in range(HALVES):
            for i in others:
                theta_copy(h, i).wait()
            theta_two[:docs, side(h)], theta_two[docs:, side(h)] = split(theta_all[h])
        products(turn)
        if sweep == 0:
            for i in range(1, parts):
                top_copy(i).wait()
            peak = tops[0]
            for i in range(1, parts):
                peak = jnp.maximum(peak, tops[i])
            for i in range(parts):
                scale[i] = jnp.exp(tops[i] - peak)
        if sweep < ITERS:
            sums[...] = jnp.zeros_like(sums)
            first_sums(turn)
            for i in others:
                sums_copy(0, i).start()
            for h in range(1, HALVES):
                later_sums(h)
                for i in others:
                    sums_copy(h, i).start()
            for h in range(HALVES):
                total = sums[h, mine, :]
                for i in others:
                    sums_copy(h, i).wait_recv()
                    total = total + sums_in[h, i]
                renewed = prior_ref[:, side(h)] + theta_mine[h] * total
                if sweep == ITERS - 1:
                    gamma_out[:, side(h)] = renewed
                send_theta(h, renewed)
            for h in range(HALVES):
                for i in others:
                    sums_copy(h, i).wait_send()
        else:
            def finish(q, carry):
                new_weights(turn, q)
                return lax.fori_loop(0, block, lambda j, c: spread(q * block + j, c), carry, unroll=4)

            lax.fori_loop(0, blocks, finish, 0)
    high[tokens:, :] = jnp.zeros((PIECE, cols), high.dtype)
    low[tokens:, :] = jnp.zeros((PIECE, cols), low.dtype)


def run_sweeps(found, docs, count, gamma_init, topic_prior):
    owners, parts = lax.axis_size("docs"), lax.axis_size("topics")
    (padded, cols), doc_rows, tokens = found.shape, gamma_init.shape[0], docs.shape[0]
    all_docs, lines, half = owners * doc_rows, tokens // LANES, cols // HALVES
    blocks = tokens // DEEP
    vmem = pl.BlockSpec(memory_space=pltpu.VMEM)
    f32, bf16, dma = jnp.float32, jnp.bfloat16, pltpu.SemaphoreType.DMA
    return pl.pallas_call(
        functools.partial(sweep_kernel, owners, parts),
        out_shape=(
            jax.ShapeDtypeStruct((doc_rows, cols), f32),
            jax.ShapeDtypeStruct((padded, cols), bf16),
            jax.ShapeDtypeStruct((padded, cols), bf16),
        ),
        in_specs=[vmem] * 5,
        out_specs=(vmem,) * 3,
        scratch_shapes=[
            pltpu.VMEM((lines, LANES), f32),
            pltpu.VMEM((2 * all_docs, cols), bf16),
            pltpu.VMEM((blocks, 2 * all_docs, DEEP), bf16),
            pltpu.VMEM((HALVES, all_docs, half), f32),
            pltpu.VMEM((HALVES, all_docs, half), f32),
            pltpu.VMEM((HALVES, doc_rows, half), f32),
            pltpu.VMEM((HALVES, owners, doc_rows, half), f32),
            pltpu.VMEM((parts, lines, LANES), f32),
            pltpu.VMEM((2, parts, lines, LANES), f32),
            pltpu.VMEM((parts, lines, LANES), f32),
            dma((HALVES, owners)), dma((HALVES, owners)), dma((HALVES, owners)), dma((HALVES, owners)),
            dma((parts,)), dma((parts,)), dma((2, parts, blocks)), dma((2, parts, blocks)),
        ],
        compiler_params=pltpu.CompilerParams(
            collective_id=0, has_side_effects=True,
            vmem_limit_bytes=SWEEP_LIMIT + 4 * all_docs * tokens,
        ),
    )(found, docs.reshape(lines, LANES), count.reshape(lines, LANES), gamma_init, topic_prior[None, :])


def stats_kernel(bound_ref, row_ref, high_ref, low_ref, out_ref, table, held, sems):
    depth, height, cols = held.shape
    steps = out_ref.shape[0] // height
    parts = height // SUB
    make_windows(row_ref, table)
    lane_row = lax.broadcasted_iota(jnp.int32, (SUB, PIECE), 0)

    def copy(s):
        slot = lax.rem(s, depth)
        rows = pl.ds(pl.multiple_of(s * height, height), height)
        return pltpu.make_async_copy(held.at[slot], out_ref.at[rows], sems.at[slot])

    def spread(s, part, start):
        base = (s * parts + part) * SUB
        hit = jnp.where(lane_row == window_rows(table, start) - base, 1.0, 0.0).astype(jnp.bfloat16)
        place = pl.ds(pl.multiple_of(start, STEP), PIECE)
        both = jnp.concatenate([high_ref[place, :], low_ref[place, :]], axis=0)
        return nn(jnp.concatenate([hit, hit], axis=1), both)

    def step(s, carry):
        slot = lax.rem(s, depth)

        @pl.when(s >= depth)
        def _():
            copy(s - depth).wait()

        firsts = []
        for part in range(parts):
            firsts.append(bound_ref[s * parts + part] // STEP * STEP)
            held[slot, part * SUB:(part + 1) * SUB, :] = spread(s, part, firsts[-1])
        for part in range(parts):
            end = bound_ref[s * parts + part + 1]

            def more(i, carry, part=part):
                held[slot, part * SUB:(part + 1) * SUB, :] += spread(s, part, firsts[part] + i * PIECE)
                return carry

            lax.fori_loop(1, (end - firsts[part] + PIECE - 1) // PIECE, more, 0)
        copy(s).start()
        return carry

    lax.fori_loop(0, steps, step, 0)
    for s in range(steps - depth, steps):
        copy(s).wait()


def write_stats(bounds, rows, high, low, total):
    padded, cols = high.shape
    vmem = pl.BlockSpec(memory_space=pltpu.VMEM)
    height = 512
    depth = min(8, total // height)
    return pl.pallas_call(
        stats_kernel,
        out_shape=jax.ShapeDtypeStruct((total, cols), jnp.float32),
        in_specs=[pl.BlockSpec(memory_space=pltpu.SMEM), vmem, vmem, vmem],
        out_specs=pl.BlockSpec(memory_space=pl.ANY),
        scratch_shapes=[
            pltpu.VMEM(((padded - PIECE) // STEP, PIECE), jnp.int32),
            pltpu.VMEM((depth, height, cols), jnp.float32),
            pltpu.SemaphoreType.DMA((depth,)),
        ],
        compiler_params=pltpu.CompilerParams(vmem_limit_bytes=STATS_LIMIT),
    )(bounds, rows, high, low)


def per_device(log_beta, gamma_init, topic_prior, word_block, word_row, counts):
    doc_rows, length = counts.shape
    vocab = log_beta.shape[0]
    all_docs = lax.axis_size("docs") * doc_rows
    slots = 2 * doc_rows * length

    packed = (word_block[:, :, 0] * vocab + word_row) * 4 + counts
    key = lax.sort(share_tokens(packed, vocab).reshape(-1))[:slots]
    blank = vocab * all_docs * 4
    rows = jnp.minimum(key // (4 * all_docs), vocab - 1)
    docs = (key // 4) % all_docs
    count = jnp.where(key < blank, key % 4, 0).astype(jnp.float32)
    limits = jnp.arange(0, vocab + 1, SUB, dtype=jnp.int32) * (all_docs * 4)
    bounds = jnp.sum(key[None, :] < limits[:, None], axis=1, dtype=jnp.int32)
    lines = jnp.pad(rows.reshape(slots // PIECE, PIECE), ((0, 8), (0, 0)), constant_values=-1)

    found = gather_rows(log_beta, lines, bounds)
    doc_gamma, high, low = run_sweeps(found, docs, count, gamma_init, topic_prior)
    sstats = write_stats(bounds, lines, high, low, vocab)
    return (doc_gamma, sstats)


def solution(mesh):
    in_specs = (
        P("docs", "topics"),
        P("docs", "topics"),
        P("topics"),
        P("docs", None, None),
        P("docs", None),
        P("docs", None),
    )
    out_specs = (P("docs", "topics"), P("docs", "topics"))
    return jax.shard_map(
        per_device, mesh=mesh, in_specs=in_specs, out_specs=out_specs, check_vma=False
    )
```

profile of v0, /device:TPU:0, one launch (start us, length us, event | category | flops | bytes accessed | tf_op | source)
XLA Modules:
  0.0 156.7 jit_solution(17692170964973009167)
XLA Ops:
  0.6 1.4 fusion.10.packed_ref
  2.0 10.7 %shard_map.77 = s32[128,256]{1,0:T(8,128)} custom-call(s32[16,256]{1,0:T(8,128)} %fusion.10.packed_ref), custom_call_target="tpu_custom_call" | custom-call | tf_op jit(solution)/shard_map/pallas_call | solution.py:60
  12.7 1.0 copy.10
  13.7 11.2 %sort.14 = (s32[32768]{0:T(1024)S(1)}, s32[32768]{0:T(1024)}) sort(s32[32768]{0:T(1024)S(1)} %bitcast.26, s32[32768]{0:T(1024)S(1)} %iota.8), dimensions={0}, to_apply=%region_0.0 | sort | flops 491520 | bytes 524288 | tf_op jit(solution)/shard_map/sort | solution.py:497
  24.9 0.7 convert_reduce_fusion.bound_ref
  25.6 0.1 fusion.4
  25.7 0.0 copy-start
  25.7 0.0 copy-start.1
  25.7 15.0 %shard_map.78.found_ref = bf16[8320,512]{1,0:T(8,128)(2,1)S(1)} custom-call(s32[129]{0:T(256)S(1)} %convert_reduce_fusion.bound_ref, s32[72,128]{1,0:T(8,128)S(1)} %pad.4.row_ref, bf16[32768,512]{1,0:T(8,128)(2,1)} %beta_ref.1), custom_call_target="tpu_custom_call" | custom-call | tf_op jit(solution)/shard_map/pallas_call | solution.py:143
  40.8 0.0 copy-done
  40.8 0.0 copy-done.1
  40.8 91.9 %shard_map.79 = (f32[16,512]{1,0:T(8,128)S(1)}, bf16[8320,512]{1,0:T(8,128)(2,1)S(1)}, bf16[8320,512]{1,0:T(8,128)(2,1)S(1)}) custom-call(bf16[8320,512]{1,0:T(8,128)(2,1)S(1)} %shard_map.78.found_ref, s32[32,256]{1,0:T(8,128)S(1)} %get-tuple-element.12.doc_ref, f32[32,256]{1,0:T(8,128)S(1)} %get-tuple-element.11.count_ref, f32[16,512]{1,0:T(8,128)S(1)} %copy-done, ...), custom_call_target="tpu_custom_call" | custom-call | tf_op jit(solution)/shard_map/pallas_call | solution.py:395
  132.7 23.4 %shard_map.80 = f32[32768,512]{1,0:T(8,128)} custom-call(s32[129]{0:T(256)S(1)} %convert_reduce_fusion.bound_ref, s32[72,128]{1,0:T(8,128)S(1)} %pad.4.row_ref, bf16[8320,512]{1,0:T(8,128)(2,1)S(1)} %get-tuple-element.9.high_ref, bf16[8320,512]{1,0:T(8,128)(2,1)S(1)} %get-tuple-element.10.low_ref), custom_call_target="tpu_custom_call" | custom-call | tf_op jit(solution)/shard_map/pallas_call | solution.py:476
  156.1 0.6 copy.15
  (6 shorter events, 0.1 us)
Async XLA Ops:
  25.7 15.1 %copy-start = (f32[16,512]{1,0:T(8,128)S(1)}, f32[16,512]{1,0:T(8,128)}, u32[]{:S(2)}) copy-start(f32[16,512]{1,0:T(8,128)} %gamma_ref.1) | copy-start | bytes 98308
  25.7 15.1 %copy-start.1 = (f32[512]{0:T(512)S(1)}, f32[512]{0:T(512)}, u32[]{:S(2)}) copy-start(f32[512]{0:T(512)} %param.8) | copy-start | bytes 6148
where the time goes:
time: 157 us
  Pallas kernels  141 us (90%)
  other arithmetic  13.3 us (8%)
  local copies, waits for them, and re-layouts  1.64 us (1%)
    pallas_call x1, Pallas kernels, run_sweeps(): pl.pallas_call(functools.partial(sweep_kernel, owners, parts), out_shape=...  91.9 us
    pallas_call x1, Pallas kernels, write_stats(): pl.pallas_call(stats_kernel, out_shape=jax.ShapeDtypeStruct((total, cols)...  23.4 us
    pallas_call x1, Pallas kernels, gather_rows(): pl.pallas_call(gather_kernel, out_shape=jax.ShapeDtypeStruct((slots + PIE...  15 us
    sort x1, other arithmetic, per_device(): key = lax.sort(share_tokens(packed, vocab).reshape(-1))[:slots]  11.2 us
    pallas_call x1, Pallas kernels, share_tokens(): pl.pallas_call(functools.partial(share_kernel, owners, vocab), out_shape=...  10.7 us

commit v1 on v0

--- a/solution.py
+++ b/solution.py
@@ -138,8 +138,8 @@
 
 def gather_rows(log_beta, rows, bounds):
     (total, cols), slots = log_beta.shape, (rows.shape[0] - 8) * PIECE
-    height = 1024
-    depth = min(8, total // height)
+    height = 2048
+    depth = min(4, total // height)
     return pl.pallas_call(
         gather_kernel,
         out_shape=jax.ShapeDtypeStruct((slots + PIECE, cols), log_beta.dtype),
@@ -471,8 +471,8 @@
 def write_stats(bounds, rows, high, low, total):
     padded, cols = high.shape
     vmem = pl.BlockSpec(memory_space=pltpu.VMEM)
-    height = 512
-    depth = min(8, total // height)
+    height = 1024
+    depth = min(4, total // height)
     return pl.pallas_call(
         stats_kernel,
         out_shape=jax.ShapeDtypeStruct((total, cols), jnp.float32),

time: 157 us -> 154 us (0.981)
  Pallas kernels: 141 us -> 137 us
    pallas_call x1, Pallas kernels: 15 us -> 12.5 us  [gather_rows(): pl.pallas_call(gather_kernel, out_shape=jax.ShapeDtypeStruct((slots + PIE...]
where the time goes in v1:
time: 154 us; the launch traced here: 153 us
  Pallas kernels  137 us (89%)
  other arithmetic  13.3 us (9%)
  local copies, waits for them, and re-layouts  1.64 us (1%)
    pallas_call x1, Pallas kernels, run_sweeps(): pl.pallas_call(functools.partial(sweep_kernel, owners, parts), out_shape=...  92 us
    pallas_call x1, Pallas kernels, write_stats(): pl.pallas_call(stats_kernel, out_shape=jax.ShapeDtypeStruct((total, cols)...  22.2 us
    pallas_call x1, Pallas kernels, gather_rows(): pl.pallas_call(gather_kernel, out_shape=jax.ShapeDtypeStruct((slots + PIE...  12.5 us
    sort x1, other arithmetic, per_device(): key = lax.sort(share_tokens(packed, vocab).reshape(-1))[:slots]  11.2 us
    pallas_call x1, Pallas kernels, share_tokens(): pl.pallas_call(functools.partial(share_kernel, owners, vocab), out_shape=...  10.7 us

profile of v1, /device:TPU:0, one launch (start us, length us, event | category | flops | bytes accessed | tf_op | source)
XLA Modules:
  0.0 153.1 jit_solution(4104918342284954547)
XLA Ops:
  0.6 1.4 fusion.10.packed_ref
  2.0 10.7 %shard_map.77 = s32[128,256]{1,0:T(8,128)} custom-call(s32[16,256]{1,0:T(8,128)} %fusion.10.packed_ref), custom_call_target="tpu_custom_call" | custom-call | tf_op jit(solution)/shard_map/pallas_call | solution.py:60
  12.7 1.0 copy.10
  13.7 11.2 %sort.14 = (s32[32768]{0:T(1024)S(1)}, s32[32768]{0:T(1024)}) sort(s32[32768]{0:T(1024)S(1)} %bitcast.26, s32[32768]{0:T(1024)S(1)} %iota.8), dimensions={0}, to_apply=%region_0.0 | sort | flops 491520 | bytes 524288 | tf_op jit(solution)/shard_map/sort | solution.py:497
  24.9 0.7 convert_reduce_fusion.bound_ref
  25.6 0.1 fusion.4
  25.7 0.0 copy-start
  25.7 0.0 copy-start.1
  25.7 12.5 %shard_map.78.found_ref = bf16[8320,512]{1,0:T(8,128)(2,1)S(1)} custom-call(s32[129]{0:T(256)S(1)} %convert_reduce_fusion.bound_ref, s32[72,128]{1,0:T(8,128)S(1)} %pad.4.row_ref, bf16[32768,512]{1,0:T(8,128)(2,1)} %beta_ref.1), custom_call_target="tpu_custom_call" | custom-call | tf_op jit(solution)/shard_map/pallas_call | solution.py:143
  38.3 0.0 copy-done
  38.3 0.0 copy-done.1
  38.3 92.0 %shard_map.79 = (f32[16,512]{1,0:T(8,128)S(1)}, bf16[8320,512]{1,0:T(8,128)(2,1)S(1)}, bf16[8320,512]{1,0:T(8,128)(2,1)S(1)}) custom-call(bf16[8320,512]{1,0:T(8,128)(2,1)S(1)} %shard_map.78.found_ref, s32[32,256]{1,0:T(8,128)S(1)} %get-tuple-element.12.doc_ref, f32[32,256]{1,0:T(8,128)S(1)} %get-tuple-element.11.count_ref, f32[16,512]{1,0:T(8,128)S(1)} %copy-done, ...), custom_call_target="tpu_custom_call" | custom-call | tf_op jit(solution)/shard_map/pallas_call | solution.py:395
  130.3 22.2 %shard_map.80 = f32[32768,512]{1,0:T(8,128)} custom-call(s32[129]{0:T(256)S(1)} %convert_reduce_fusion.bound_ref, s32[72,128]{1,0:T(8,128)S(1)} %pad.4.row_ref, bf16[8320,512]{1,0:T(8,128)(2,1)S(1)} %get-tuple-element.9.high_ref, bf16[8320,512]{1,0:T(8,128)(2,1)S(1)} %get-tuple-element.10.low_ref), custom_call_target="tpu_custom_call" | custom-call | tf_op jit(solution)/shard_map/pallas_call | solution.py:476
  152.5 0.6 copy.15
  (6 shorter events, 0.1 us)
Async XLA Ops:
  25.7 12.6 %copy-start = (f32[16,512]{1,0:T(8,128)S(1)}, f32[16,512]{1,0:T(8,128)}, u32[]{:S(2)}) copy-start(f32[16,512]{1,0:T(8,128)} %gamma_ref.1) | copy-start | bytes 98308
  25.7 12.6 %copy-start.1 = (f32[512]{0:T(512)S(1)}, f32[512]{0:T(512)}, u32[]{:S(2)}) copy-start(f32[512]{0:T(512)} %param.8) | copy-start | bytes 6148
